TPU v7x, 256 devices: a whole 4x4x8 slice. The times are simulated.
256 devices in a mesh: dp: 256 (over y, z, x, core).
Axes of the slice: x: 4, y: 4, z: 8, core: 2. Of those that a mesh axis runs over, the one named last changes fastest.
Arguments:
- master: float32 [524288], P('dp'), may hold values from -6 to 6
- gradients: float32 [524288], P('dp'), may hold values from -6 to 6
- first_moment: float32 [524288], P('dp'), may hold values from -4 to 4
- second_moment: float32 [524288], P('dp'), may hold values from 0.01 to 1
- segment_ids: int32 [524288], P('dp'), may hold values from 0 to 511, as said below
- decay_mask: int32 [512], replicated, may hold values 0 or 1
Outputs:
- new_master: float32 [524288], P('dp')
- new_first: float32 [524288], P('dp')
- new_second: float32 [524288], P('dp')
- scaled_step: float32 [524288], P('dp')
- model_weights: bfloat16 [524288], replicated
Inputs may be any that keep to these rules, and one draw needn't show every extreme that they name: segment_ids never falls along the flat vector; each tensor 0 to 511 owns one contiguous run of 256 to 16384 elements, and one tensor has exactly 16384. `decay_mask`: each entry is 0 or 1.
All inputs are finite; a program needn't handle non-finite values.
Results may differ from a plain program's by a relative error of at most 0.0004.
Values may be sent and summed in bfloat16 or wider, within the bound.
A program may use at most 64 MiB of HBM per device.

v0:
```python
import functools
import math
import jax
import jax.numpy as jnp
from jax import lax
from jax.sharding import Mesh
from jax.sharding import PartitionSpec as P

SEG_DEV = 2
STEP = 20
DP = ("dp_0", "dp_1", "dp_2", "dp_3")
first_decay = 0.9
second_decay = 0.999
epsilon = 1e-06
weight_decay = 0.01
learn_rate = 0.006


def one_axis_at_a_time(value, axes):
    return functools.reduce(lax.psum, axes, value)


def adam_direction(master, gradients, first_moment, second_moment, decay):
    new_first = first_decay * first_moment + (1.0 - first_decay) * gradients
    new_second = second_decay * second_moment + (1.0 - second_decay) * gradients * gradients
    hat_first = new_first / (1.0 - first_decay**STEP)
    hat_second = new_second / (1.0 - second_decay**STEP)
    direction = hat_first / (jnp.sqrt(hat_second) + epsilon) + weight_decay * decay * master
    return (new_first, new_second, direction)


def trust_ratio(weight_sq, step_sq):
    weight_norm = jnp.sqrt(weight_sq)
    step_norm = jnp.sqrt(step_sq)
    usable = (weight_norm > 0.0) & (step_norm > 0.0)
    return jnp.where(usable, weight_norm / jnp.where(usable, step_norm, 1.0), 1.0)


def block_rows(length):
    return math.gcd(length, 1024)


def one_hot_block(ids, width):
    columns = lax.broadcasted_iota(jnp.int32, (ids.shape[0], width), 1)
    return (ids[:, None] == columns).astype(jnp.float32)


def spread(table, ids, width):
    length = ids.shape[0]
    rows = block_rows(length)
    blocks = ids.reshape(length // rows, rows)

    def one_block(block_ids):
        return jnp.dot(one_hot_block(block_ids, width), table, precision=lax.Precision.HIGHEST)

    return lax.map(one_block, blocks).reshape(length, table.shape[1])


def collect(values, ids, width):
    length = ids.shape[0]
    rows = block_rows(length)
    blocks = ids.reshape(length // rows, rows)
    value_blocks = values.reshape(length // rows, rows, values.shape[1])

    def add_block(total, pair):
        block_ids, block_values = pair
        term = lax.dot_general(
            one_hot_block(block_ids, width),
            block_values,
            (((0,), (0,)), ((), ())),
            precision=lax.Precision.HIGHEST,
        )
        return (total + term, None)

    start = jnp.zeros((width, values.shape[1]), jnp.float32)
    total, unused = lax.scan(add_block, start, (blocks, value_blocks))
    return total


def to_global(partial_value, first_id, tensors, width):
    holder = jnp.zeros((tensors + width, partial_value.shape[1]), jnp.float32)
    placed = lax.dynamic_update_slice_in_dim(holder, partial_value, first_id, 0)
    return placed[:tensors]


def to_local(table, first_id, width, filler):
    padded = jnp.concatenate([table, jnp.full((width,), filler, jnp.float32)])
    return lax.dynamic_slice_in_dim(padded, first_id, width)


def shards(master, gradients, first_moment, second_moment, segment_ids, decay_mask):
    tensors = decay_mask.shape[0]
    width = 4 * SEG_DEV + 2
    first_id = segment_ids[0].astype(jnp.int32)
    local_ids = (segment_ids - first_id).astype(jnp.int32)
    local_mask = to_local(decay_mask.astype(jnp.float32), first_id, width, 0.0)
    decay = spread(local_mask[:, None], local_ids, width)[:, 0]
    weight_square = master * master
    new_first, new_second, direction = adam_direction(
        master, gradients, first_moment, second_moment, decay
    )
    stacked = jnp.stack([weight_square, direction * direction], axis=1)
    packed_partial = to_global(collect(stacked, local_ids, width), first_id, tensors, width)
    totals = one_axis_at_a_time(packed_partial, DP)
    ratios = to_local(trust_ratio(totals[:, 0], totals[:, 1]), first_id, width, 1.0)
    per_element = spread(ratios[:, None], local_ids, width)[:, 0]
    scaled_step = per_element * direction
    new_master = master - learn_rate * scaled_step
    model_weights = lax.all_gather(new_master.astype(jnp.bfloat16), DP, axis=0, tiled=True)
    return (new_master, new_first, new_second, scaled_step, model_weights)


def solution(mesh):
    torus = Mesh(mesh.devices.reshape(4, 8, 4, 2), ("dp_0", "dp_1", "dp_2", "dp_3"))
    return jax.shard_map(
        shards,
        mesh=torus,
        in_specs=(P(DP), P(DP), P(DP), P(DP), P(DP), P()),
        out_specs=(P(DP), P(DP), P(DP), P(DP), P()),
        check_vma=False,
    )
```

profile of v0, /device:TPU:1, one launch (start us, length us, event | category | flops | bytes accessed | tf_op | source)
XLA Modules:
  0.0 167.1 jit_solution(12047578045685534841)
XLA Ops:
  7.2 0.0 copy-start.4
  7.2 0.0 all-gather.2.cloned.1.call-start
  7.2 1.2 slice.12
  9.1 0.0 copy-done.4
  9.1 0.0 copy-start.5
  9.1 0.7 broadcast_subtract_fusion
  10.4 0.0 copy-done.5
  11.1 0.1 fusion.10
  11.2 0.0 copy-start.2
  11.2 0.0 copy-start.3
  11.2 1.0 while.31
  11.2 0.5 fusion.23
  11.7 0.5 fusion.23
  12.2 0.0 copy-start
  12.2 0.0 copy-start.1
  12.2 0.0 copy-done.2
  12.2 0.0 copy-done.3
  12.2 0.7 copy-done
  12.9 0.0 copy-done.1
  12.9 0.6 fusion.13
  13.5 0.8 while.33
  13.6 0.4 convolution_add_fusion.2
  14.0 0.4 convolution_add_fusion.2
  14.4 0.3 dynamic_update_slice.10
  14.7 9.5 %psum.28 = f32[512,2]{0,1:T(2,128)S(1)} all-reduce(f32[512,2]{0,1:T(2,128)S(1)} %slice.16), channel_id=1, replica_groups=mesh['dp_0'=4,'dp_1'=8,'dp_2'=4,'dp_3'=2] {'dp_0'}, use_global_device_ids=true, to_apply=%region_4.5 | all-reduce | flops 1024 | bytes 8192 | tf_op jit(solution)/shard_map/psum | solution.py:20
  24.2 16.2 %psum.29 = f32[512,2]{0,1:T(2,128)S(1)} all-reduce(f32[512,2]{0,1:T(2,128)S(1)} %psum.28), channel_id=1, replica_groups=mesh['dp_0'=4,'dp_1'=8,'dp_2'=4,'dp_3'=2] {'dp_1'}, use_global_device_ids=true, to_apply=%region_5.6 | all-reduce | flops 1024 | bytes 8192 | tf_op jit(solution)/shard_map/psum | solution.py:20
  40.4 8.5 %psum.30 = f32[512,2]{0,1:T(2,128)S(1)} all-reduce(f32[512,2]{0,1:T(2,128)S(1)} %psum.29), channel_id=1, replica_groups=mesh['dp_0'=4,'dp_1'=8,'dp_2'=4,'dp_3'=2] {'dp_2'}, use_global_device_ids=true, to_apply=%region_6.7 | all-reduce | flops 1024 | bytes 8192 | tf_op jit(solution)/shard_map/psum | solution.py:20
  48.9 10.6 %psum.31 = f32[512,2]{0,1:T(2,128)S(1)} all-reduce(f32[512,2]{0,1:T(2,128)S(1)} %psum.30), channel_id=1, replica_groups=mesh['dp_0'=4,'dp_1'=8,'dp_2'=4,'dp_3'=2] {'dp_3'}, use_global_device_ids=true, to_apply=%region_7.8 | all-reduce | flops 1024 | bytes 8192 | tf_op jit(solution)/shard_map/psum | solution.py:20
  59.5 0.1 fusion.11
  59.6 0.9 while.32
  59.6 0.5 fusion.25
  60.1 0.5 fusion.25
  60.6 0.6 fusion.12
  61.2 0.0 all-gather.2.cloned.1.call-update
  61.2 96.8 %all-gather.2.cloned.1.call-done = bf16[524288]{0:T(1024)(128)(2,1)} async-done(((bf16[2048]{0:T(1024)(128)(2,1)}), bf16[524288]{0:T(1024)(128)(2,1)}) %all-gather.2.cloned.1.call-update) | async-done | bytes 1048592 | tf_op jit(solution)/shard_map/all_gather | solution.py:109
  158.0 2.3 %copy.35 = bf16[524288]{0:T(1024)(128)(2,1)} copy(bf16[524288]{0:T(1024)(128)(2,1)} %all-gather.2.cloned.1.call-done) | data formatting | bytes 2097152
  (17 shorter events, 0.2 us)
Async XLA Ops:
  7.2 1.9 %copy-start.4 = (s32[2048]{0:T(1024)S(1)}, s32[2048]{0:T(1024)}, u32[]{:S(2)}) copy-start(s32[2048]{0:T(1024)} %param.16) | copy-start | bytes 24580
  7.2 150.8 %all-gather.2.cloned.1.call-start = ((), (), s32[]{:S(2)}) async-start(), calls=%async_computation | async-start | bytes 1052672 | tf_op jit(solution)/shard_map/all_gather | solution.py:109
  9.1 1.3 copy-start.5
  11.2 1.0 copy-start.2
  11.2 1.0 copy-start.3
  12.2 0.7 copy-start
  12.2 0.7 copy-start.1
Sparse Core Ops, SparseCore 0:
  61.3 96.5 all-gather.1
where the time goes:
time: 167 us
  waiting for transfers between devices  96.8 us (58%)
  blocking collectives  44.8 us (27%)
  between operations  16.1 us (10%)
  local copies, waits for them, and re-layouts  4.7 us (3%)
  matrix products  2.58 us (2%)
  other arithmetic  1.93 us (1%)
    all_gather x1, waiting for transfers between devices, shards(): lax.all_gather(new_master.astype(jnp.bfloat16), DP, axis=0, tiled=True)  96.8 us
    psum x4, blocking collectives, one_axis_at_a_time(): return functools.reduce(lax.psum, axes, value)  44.8 us
  transfers between devices with their start and end apart: 1, of which 1 were waited for; matrix products, arithmetic and copies ran while one was open for 0% of the time, Pallas kernels for 0%

commit v1 on v0

--- a/solution.py
+++ b/solution.py
@@ -14,6 +14,15 @@
 epsilon = 1e-06
 weight_decay = 0.01
 learn_rate = 0.006
+raise_inputs = lambda packet, mesh_name: jnp.concatenate(
+    lax.all_to_all(
+        jnp.stack([packet for _ in range(lax.axis_size(mesh_name))], axis=0),
+        split_axis=0,
+        concat_axis=0,
+        axis_name=mesh_name,
+    ),
+    0,
+)
 
 
 def one_axis_at_a_time(value, axes):
@@ -106,7 +115,7 @@
     per_element = spread(ratios[:, None], local_ids, width)[:, 0]
     scaled_step = per_element * direction
     new_master = master - learn_rate * scaled_step
-    model_weights = lax.all_gather(new_master.astype(jnp.bfloat16), DP, axis=0, tiled=True)
+    model_weights = raise_inputs(new_master.astype(jnp.bfloat16), DP)
     return (new_master, new_first, new_second, scaled_step, model_weights)
 
 

time: 167 us -> 110 us (0.66)
  waiting for transfers between devices: 96.8 us -> 0 us
  blocking collectives: 44.8 us -> 81.2 us
  other arithmetic: 1.93 us -> 17 us
  between operations: 16.1 us -> 2.69 us
    all_gather x1 -> x0, waiting for transfers between devices: 96.8 us -> none  [shards(): lax.all_gather(new_master.astype(jnp.bfloat16), DP, axis=0, tiled=True)]
    all_to_all x0 -> x1, blocking collectives: none -> 36.3 us  [lax.all_to_all(jnp.stack([packet for _ in range(lax.axis_size(mesh_name))...]
    another operation x0 -> x1, other arithmetic: none -> 6.79 us  [jnp.stack([packet for _ in range(lax.axis_size(mesh_name))], axis=0)]
    all_to_all x0 -> x1, other arithmetic: none -> 6.15 us  [lax.all_to_all(jnp.stack([packet for _ in range(lax.axis_size(mesh_name))...]
  transfers between devices with their start and end apart: 1 -> 0, of which waited for: 1 -> 0; matrix products, arithmetic and copies ran while one was open for 0% -> 0% of each run, Pallas kernels for 0% -> 0%
where the time goes in v1:
time: 110 us
  blocking collectives  81.2 us (74%)
  other arithmetic  17 us (15%)
  local copies, waits for them, and re-layouts  6.2 us (6%)
  between operations  2.69 us (2%)
  matrix products  2.58 us (2%)
    psum x4, blocking collectives, one_axis_at_a_time(): return functools.reduce(lax.psum, axes, value)  44.8 us
    all_to_all x1, blocking collectives, lax.all_to_all(jnp.stack([packet for _ in range(lax.axis_size(mesh_name))...  36.3 us
    another operation x1, other arithmetic, jnp.stack([packet for _ in range(lax.axis_size(mesh_name))], axis=0)  6.79 us
    all_to_all x1, other arithmetic, lax.all_to_all(jnp.stack([packet for _ in range(lax.axis_size(mesh_name))...  6.15 us
    unnamed x5, local copies, waits for them, and re-layouts  2.87 us

profile of v1, /device:TPU:1, one launch (start us, length us, event | category | flops | bytes accessed | tf_op | source)
XLA Modules:
  0.0 109.7 jit_solution(16383539031392459740)
XLA Ops:
  0.6 0.0 copy-start
  0.7 1.2 %slice.12 = s32[1]{0:T(128)} slice(s32[2048]{0:T(1024)} %param.16), slice={[0:1]} | slice | bytes 8 | tf_op jit(solution)/shard_map/slice | solution.py:103
  2.5 1.3 %broadcast_subtract_fusion = s32[2048]{0:T(1024)S(1)} fusion(s32[2048]{0:T(1024)} %param.16, s32[]{:T(128)} %bitcast.8), kind=kLoop, calls=%fused_computation.26 | loop fusion | flops 2048 | bytes 16388 | tf_op jit(solution)/shard_map/sub | solution.py:104
  4.5 0.7 convert_element_type.7
  5.9 0.1 fusion.10
  5.9 0.9 while.31
  6.0 0.5 fusion.23
  6.4 0.5 fusion.23
  6.9 1.4 %fusion.13 = (f32[2048]{0:T(1024)S(1)}, f32[2048]{0:T(1024)S(1)}, f32[2048]{0:T(1024)}, f32[2048]{0:T(1024)}, f32[2048]{0:T(1024)S(1)}) fusion(f32[2048]{0:T(1024)S(1)} %bitcast.56, f32[2048]{0:T(1024)} %param.12, f32[2048]{0:T(1024)} %param.13, f32[2048]{0:T(1024)} %param.14, f32[2048]{0:T(1024)} %param.15), kind=kLoop, calls=%fused_computation.34 | loop fusion | flops 30720 | bytes 81920 | tf_op jit(solution)/shard_map/mul | solution.py:111
  8.3 0.8 while.33
  8.3 0.4 convolution_add_fusion.2
  8.7 0.4 convolution_add_fusion.2
  9.2 0.3 dynamic_update_slice.10
  9.4 9.5 %psum.28 = f32[512,2]{0,1:T(2,128)S(1)} all-reduce(f32[512,2]{0,1:T(2,128)S(1)} %slice.16), channel_id=1, replica_groups=mesh['dp_0'=4,'dp_1'=8,'dp_2'=4,'dp_3'=2] {'dp_0'}, use_global_device_ids=true, to_apply=%region_4.5 | all-reduce | flops 1024 | bytes 8192 | tf_op jit(solution)/shard_map/psum | solution.py:29
  19.0 16.2 %psum.29 = f32[512,2]{0,1:T(2,128)S(1)} all-reduce(f32[512,2]{0,1:T(2,128)S(1)} %psum.28), channel_id=1, replica_groups=mesh['dp_0'=4,'dp_1'=8,'dp_2'=4,'dp_3'=2] {'dp_1'}, use_global_device_ids=true, to_apply=%region_5.6 | all-reduce | flops 1024 | bytes 8192 | tf_op jit(solution)/shard_map/psum | solution.py:29
  35.2 8.5 %psum.30 = f32[512,2]{0,1:T(2,128)S(1)} all-reduce(f32[512,2]{0,1:T(2,128)S(1)} %psum.29), channel_id=1, replica_groups=mesh['dp_0'=4,'dp_1'=8,'dp_2'=4,'dp_3'=2] {'dp_2'}, use_global_device_ids=true, to_apply=%region_6.7 | all-reduce | flops 1024 | bytes 8192 | tf_op jit(solution)/shard_map/psum | solution.py:29
  43.7 10.6 %psum.31 = f32[512,2]{0,1:T(2,128)S(1)} all-reduce(f32[512,2]{0,1:T(2,128)S(1)} %psum.30), channel_id=1, replica_groups=mesh['dp_0'=4,'dp_1'=8,'dp_2'=4,'dp_3'=2] {'dp_3'}, use_global_device_ids=true, to_apply=%region_7.8 | all-reduce | flops 1024 | bytes 8192 | tf_op jit(solution)/shard_map/psum | solution.py:29
  54.3 0.1 fusion.11
  54.4 0.9 while.32
  54.4 0.5 fusion.25
  54.9 0.5 fusion.25
  55.3 0.0 copy-done
  55.3 0.6 fusion.12
  56.0 1.1 stack.11
  57.1 0.5 broadcast.34
  57.6 6.8 %reduce.1 = bf16[256,2048]{1,0:T(8,128)(2,1)S(1)} reduce(bf16[256,1,2048]{2,1,0:T(2,128)(2,1)S(1)} %stack.11, bf16[]{:T(256)} %broadcast.34), dimensions={1}, to_apply=%stack.11.reduce_sub_computation | reduce | bytes 2097154 | tf_op jit(solution)/shard_map/stack | solution.py:19
  64.4 0.8 reshape.58
  65.2 36.3 %all_to_all.6 = bf16[256,2,1024]{2,1,0:T(2,128)(2,1)S(1)} all-to-all(bf16[256,2,1024]{2,1,0:T(2,128)(2,1)S(1)} %reshape.58), channel_id=1, replica_groups=mesh['dp_0'=4,'dp_1'=8,'dp_2'=4,'dp_3'=2] {'dp_0','dp_1','dp_2','dp_3'}, dimensions={0} | all-to-all | bytes 2097152 | tf_op jit(solution)/shard_map/all_to_all | solution.py:18
  101.5 0.9 reshape.59
  102.4 6.2 %reduce = bf16[256,2048]{1,0:T(8,128)(2,1)S(1)} reduce(bf16[256,1,2048]{2,1,0:T(2,128)(2,1)S(1)} %reshape.59, bf16[]{:T(256)} %constant.61), dimensions={1}, to_apply=%all_to_all.4.reduce_sub_computation | reduce | bytes 2097154 | tf_op jit(solution)/shard_map/all_to_all | solution.py:18
  108.5 1.2 %copy.11 = bf16[32,16,8,128]{3,1,2,0:T(8,128)(2,1)} copy(bf16[32,16,8,128]{3,2,1,0:T(8,128)(2,1)S(1)} %bitcast.51) | data formatting | bytes 2097152
  (16 shorter events, 0.2 us)
Async XLA Ops:
  0.6 54.7 %copy-start = (f32[2048]{0:T(1024)S(1)}, f32[2048]{0:T(1024)}, u32[]{:S(2)}) copy-start(f32[2048]{0:T(1024)} %param.12) | copy-start | bytes 24580
